TPU v7x, 32 devices: a whole 2x2x4 slice. The times are simulated.
32 devices in a mesh: gz: 4 (over y, x), gy: 4 (over z), gx: 2 (over core).
Axes of the slice: x: 2, y: 2, z: 4, core: 2. Of those that a mesh axis runs over, the one named last changes fastest.
Arguments:
- spins: float32 [2, 64, 192, 256], P(None, 'gz', 'gy', 'gx'), may hold values from -6 to 6
- kicks: float32 [2, 2, 64, 192, 256], P(None, None, 'gz', 'gy', 'gx'), may hold values from -6 to 6
- stiffness: float32 [64, 192, 256], P('gz', 'gy', 'gx'), may hold values from 0.1 to 11, as said below
Outputs:
- final_spins: float32 [2, 64, 192, 256], P(None, 'gz', 'gy', 'gx')
- section_energy: float32 [16], replicated
Inputs may be any that keep to these rules, and one draw needn't show every extreme that they name: `stiffness`: positive coupling strengths.
All inputs are finite; a program needn't handle non-finite values.
Results may differ from a plain program's by a relative error of at most 0.0001.
Values sent between devices are 32-bit elements; how exact they have to be, the bound alone decides.
No kernel may reach another device: no remote copies, remote signals or barrier semaphores. Data moves between devices by JAX's collectives and lax.ppermute only.
A program may use at most 128 MiB of HBM per device.

v0:
```python
import functools

import jax
import jax.numpy as jnp
from jax import lax
from jax.experimental import pallas as pl
from jax.experimental.pallas import tpu as pltpu
from jax.sharding import PartitionSpec as P


SWEEPS = 2
FACE_GRANT = 56_000_000
EDGE_GRANT = 8_000_000
VMEM = pl.BlockSpec(memory_space=pltpu.VMEM)
F32 = jnp.float32

FIRST = (0, 1, 2, 3, 4)
ALL = (0, 1, 2, 3, 4, 5, 6)


def up_planes(depth):
    return [(f, z) for f in FIRST for z in (depth - 2, depth - 1)]


def down_planes():
    return [(f, z) for f in FIRST for z in (0, 1, 2)] + [(5, 0), (6, 0)]


CORNERS = {"cuu": (0, 1), "cud": (1, 2), "cdu": (3, 3), "cdd": (6, 5)}
CORNER_TILES = 11


def corner_rows(name):
    if name == "cuu":
        spins, first, second = {1: (-1, -2), 0: (-1,)}, {}, ()
    elif name == "cud":
        spins, first, second = {1: (0, 1, 2), 0: (0, 1)}, {1: (0,), 0: (0,)}, ()
    elif name == "cdu":
        spins, first, second = {0: (-1, -2, -3), 1: (-1, -2), 2: (-1,)}, {0: (-1, -2)}, ()
    else:
        spins, first, second = {0: (0, 1, 2, 3), 1: (0, 1, 2), 2: (0, 1)}, {0: (0, 1, 2), 1: (0,), 2: (0,)}, (0,)
    planes = 2 if name[1] == "u" else 3
    listed = [(planes * f + z, r) for f in FIRST for z, rows in (spins if f < 2 else first).items() for r in rows]
    return listed + [(n, r) for n in (15, 16) for r in second]


def load_field(s_ref, k_ref, st_ref, field, z, rows=slice(None)):
    return field_ref(s_ref, k_ref, st_ref, field)[z, rows, :]


def field_ref(s_ref, k_ref, st_ref, field):
    if field < 2:
        return s_ref.at[field]
    if field == 2:
        return st_ref
    return k_ref.at[(field - 3) // 2, (field - 3) % 2]


def copy_all(moves, sems):
    copies = [pltpu.make_async_copy(a, b, sems.at[i]) for i, (a, b) in enumerate(moves)]
    for c in copies:
        c.start()
    for c in copies:
        c.wait()


def face_kernel(s_ref, k_ref, st_ref, zup, zdn, far, sems):
    depth, _, _ = st_ref.shape
    get = functools.partial(field_ref, s_ref, k_ref, st_ref)
    moves = [(s_ref.at[:, depth - 3], far.at[0]), (s_ref.at[:, 3], far.at[1])]
    for f in FIRST:
        moves.append((get(f).at[pl.ds(0, 3)], zdn.at[pl.ds(3 * f, 3)]))
        moves.append((get(f).at[pl.ds(depth - 2, 2)], zup.at[pl.ds(2 * f, 2)]))
    moves += [(get(5).at[pl.ds(0, 1)], zdn.at[pl.ds(15, 1)]), (get(6).at[pl.ds(0, 1)], zdn.at[pl.ds(16, 1)])]
    copy_all(moves, sems)
    for c in (0, 1):
        n = 2 * (3 + c)
        zup[n] = zup[n] + zup[4] * far[0, c]
        n = 3 * (3 + c) + 2
        zdn[n] = zdn[n] + zdn[8] * far[1, c]


def edge_kernel(s_ref, k_ref, st_ref, zup, zdn, up, down, corners, s_low, s_high, k_low, k_high, t_low, t_high, sems):
    depth, height, lanes = st_ref.shape
    first, last = pl.ds(0, 8), pl.ds(height - 8, 8)
    copy_all(
        [
            (s_ref.at[:, :, first], s_low),
            (s_ref.at[:, :, last], s_high),
            (k_ref.at[:, :, :, first], k_low),
            (k_ref.at[0, :, :, last], k_high),
            (st_ref.at[:, first], t_low),
            (st_ref.at[:, last], t_high),
        ],
        sems,
    )
    sub = lax.broadcasted_iota(jnp.int32, (8, lanes), 0)
    quad = sub % 4
    order = (quad % 2) * 2 + quad // 2
    lower = sub < 4

    def merge(a, b, base):
        a = jnp.take_along_axis(a, order + base, axis=0)
        b = jnp.take_along_axis(b, order + base, axis=0)
        return jnp.where(lower, a, b)

    for name, (start, count) in CORNERS.items():
        src = zup if name[1] == "u" else zdn
        tiles = [jnp.zeros((8, lanes), F32)] * count
        for i, (n, r) in enumerate(corner_rows(name)):
            value, place = (src[n, first, :], r) if r >= 0 else (src[n, last, :], 8 + r)
            shift = (i - place) % 8
            value = pltpu.roll(value, shift, 0) if shift else value
            tiles[i // 8] = jnp.where(sub == i % 8, value, tiles[i // 8])
        for i in range(count):
            corners[start + i] = tiles[i]

    def row(field, z, is_low):
        s, k, t = (s_low, k_low, t_low) if is_low else (s_high, k_high, t_high)
        if field < 2:
            return s[field, z]
        if field == 2:
            return t[z]
        c = (field - 3) % 2
        if not is_low:
            return k[c, z] + jnp.where(sub == 6, t[z] * pltpu.roll(s[c, z], 1, 0), 0.0)
        if field > 4:
            return k[1, c, z]
        return k[0, c, z] + jnp.where(sub == 2, t[z] * pltpu.roll(s[c, z], 7, 0), 0.0)

    for field in FIRST:
        for p in range(depth // 2):
            tile = merge(row(field, 2 * p, True), row(field, 2 * p + 1, True), 0)
            if field < 2:
                a, b = (pltpu.roll(row(5 + field, 2 * p + i, True), 3 + 4 * i, 0) for i in (0, 1))
                tile = jnp.where(quad == 3, jnp.where(lower, a, b), tile)
            down[field * (depth // 2) + p] = tile
        for q in range(depth // 4):
            tile = row(field, 4 * q + 3, False)
            for i in range(3):
                tile = jnp.where(sub // 2 == i, pltpu.roll(row(field, 4 * q + i, False), (2 * i + 2) % 8, 0), tile)
            up[field * (depth // 4) + q] = tile


def pack_faces(spins, kicks, stiffness):
    _, height, lanes = stiffness.shape
    return pl.pallas_call(
        face_kernel,
        out_shape=[jax.ShapeDtypeStruct((n, height, lanes), F32) for n in (10, 17)],
        in_specs=[pl.BlockSpec(memory_space=pltpu.HBM)] * 3,
        out_specs=[VMEM] * 2,
        scratch_shapes=[pltpu.VMEM((2, 2, height, lanes), F32), pltpu.SemaphoreType.DMA((14,))],
        compiler_params=pltpu.CompilerParams(vmem_limit_bytes=FACE_GRANT),
        cost_estimate=pl.CostEstimate(flops=1_000_000, bytes_accessed=1_000_000, transcendentals=0),
        name="faces",
    )(spins, kicks, stiffness)


def pack_edges(spins, kicks, stiffness, zup, zdn):
    depth, _, lanes = stiffness.shape
    return pl.pallas_call(
        edge_kernel,
        out_shape=[jax.ShapeDtypeStruct((n, 8, lanes), F32) for n in (5 * depth // 4, 5 * depth // 2, CORNER_TILES)],
        in_specs=[pl.BlockSpec(memory_space=pltpu.HBM)] * 3 + [VMEM] * 2,
        out_specs=[VMEM] * 3,
        scratch_shapes=[
            pltpu.VMEM((2, depth, 8, lanes), F32),
            pltpu.VMEM((2, depth, 8, lanes), F32),
            pltpu.VMEM((SWEEPS, 2, depth, 8, lanes), F32),
            pltpu.VMEM((2, depth, 8, lanes), F32),
            pltpu.VMEM((depth, 8, lanes), F32),
            pltpu.VMEM((depth, 8, lanes), F32),
            pltpu.SemaphoreType.DMA((6,)),
        ],
        compiler_params=pltpu.CompilerParams(vmem_limit_bytes=EDGE_GRANT),
        cost_estimate=pl.CostEstimate(flops=1_000_000, bytes_accessed=2_000_000, transcendentals=0),
        name="edges",
    )(spins, kicks, stiffness, zup, zdn)


def small_call(kernel, shapes, *args):
    return pl.pallas_call(
        kernel,
        out_shape=[jax.ShapeDtypeStruct(s, F32) for s in shapes],
        in_specs=[VMEM] * len(args),
        out_specs=[VMEM] * len(shapes),
        compiler_params=pltpu.CompilerParams(vmem_limit_bytes=4 << 20),
        cost_estimate=pl.CostEstimate(flops=100_000, bytes_accessed=1_000_000, transcendentals=0),
    )(*args)


def per_core(moves):
    core = lax.axis_index("gx") % 2
    for c in (0, 1):

        @pl.when(core == c)
        def _():
            for target, at, source, start, count in moves[c]:
                target[at : at + count] = source[start : start + count]


def share_out(lanes, mine, pair):
    def spread(mine, pair, first, second):
        moves = ([], [])
        for core, parts in ((0, (("cdd", first), ("cud", second))), (1, (("cdu", first), ("cuu", second)))):
            for name, target in parts:
                start, count = CORNERS[name]
                moves[core].append((target, 0, mine, start, count))
                moves[core].append((target, target.shape[0] // 2, pair, start, count))
        per_core(moves)

    return small_call(spread, [(10, 8, lanes), (4, 8, lanes)], mine, pair)


def join(lo, hi):
    def join_edges(lo, hi, out):
        out[: lo.shape[0]] = lo[...]
        out[lo.shape[0] :] = hi[...]

    return small_call(join_edges, [(lo.shape[0] + hi.shape[0], *lo.shape[1:])], lo, hi)[0]


def stack_corners(lanes, first, second):
    def stack(first, second, out):
        out[:10] = first[...]
        out[10:] = second[...]

    return small_call(stack, [(14, 8, lanes)], first, second)[0]


def sort_corners(lanes, got, pair):
    def sort_c(got, pair, own, other):
        moves = ([], [])
        for name, start, half, core in (("cdd", 0, 5, 0), ("cdu", 0, 5, 1), ("cud", 10, 2, 0), ("cuu", 10, 2, 1)):
            place, count = CORNERS[name]
            for c in (0, 1):
                source, flip = (got, 0) if c == core else (pair, half)
                moves[c].append((own, place, source, start + flip, count))
                moves[c].append((other, place, source, start + half - flip, count))
        per_core(moves)

    return small_call(sort_c, [(CORNER_TILES, 8, lanes)] * 2, got, pair)


class Rows:
    def __init__(self, S, ST, K, depth, height):
        self.S, self.ST, self.K = S, ST, K
        self.depth, self.height = depth, height
        self.half = height // 2
        self.rows, self.lanes = S.shape[4:]
        lane = lax.broadcasted_iota(jnp.int32, (8, self.lanes), 1)
        self.lane = lane
        self.sub = lax.broadcasted_iota(jnp.int32, (8, self.lanes), 0)
        self.even = lax.broadcasted_iota(jnp.int32, (self.rows, self.lanes), 1) % 2 == 0
        end = self.lanes - 1
        before = jnp.where(lane == 0, 0, jnp.where(lane == 1, end, lane - 1))
        after = jnp.where(lane == 0, 0, jnp.where(lane == end, 1, lane + 1))
        self.before = jnp.concatenate([before] * (self.rows // 8), axis=0)
        self.after = jnp.concatenate([after] * (self.rows // 8), axis=0)

    def put(self, field, zi, y, start, a, b):
        b = pltpu.roll(b, 1, 1)
        even = self.even[: a.shape[0]]
        for x in (0, 1):
            value = jnp.where(even, a, b) if x == 0 else jnp.where(even, b, a)
            at = (y, x, zi, pl.ds(start, a.shape[0]))
            if field < 2:
                self.S[(field, *at)] = value
            elif field == 2:
                self.ST[at] = value
            else:
                self.K[(field - 3, *at)] = value

    def corner(self, tiles, names, n, y):
        value = jnp.zeros((8, self.lanes), F32)
        for name in names:
            for i, (m, r) in enumerate(corner_rows(name)):
                if m == n and r % 2 == y:
                    place = r // 2 if r >= 0 else {-1: 7, -2: 7, -3: 6}[r]
                    tile = tiles[CORNERS[name][0] + i // 8]
                    shift = (place - i) % 8
                    tile = pltpu.roll(tile, shift, 0) if shift else tile
                    value = jnp.where(self.sub == place, tile, value)
        return value

    def rows_beyond(self, hi, lo, j, y, second_kick):
        base = 4 * (j % 2)
        if second_kick:
            return pltpu.roll(hi, (-base - 3) % 8, 0) if y == 0 else jnp.zeros(hi.shape, F32)
        above, below = (-base - 2 * y) % 8, 7 - 2 * j - y
        above = pltpu.roll(hi, above, 0) if above else hi
        below = pltpu.roll(lo, below % 8, 0) if below % 8 else lo
        return jnp.where(self.sub < 2 - y, above, jnp.where(self.sub == 7, below, 0.0))

    def section(self, t, planes):
        S, ST, K = self.S, self.ST, self.K
        sweep, colour = divmod(t, 8)
        yp, xp = (colour // 2) % 2, colour % 2
        acc = jnp.zeros((8, self.lanes), F32)
        for z in planes:
            zi = z + 3
            stiff = ST[yp, xp, zi]
            local = []
            for c in (0, 1):
                along = S[c, yp, 1 - xp, zi]
                if xp == 0:
                    total = jnp.take_along_axis(along, self.before, axis=1) + pltpu.roll(along, self.lanes - 1, 1)
                else:
                    total = jnp.take_along_axis(along, self.after, axis=1) + pltpu.roll(along, 1, 1)
                across = S[c, 1 - yp, xp, zi]
                total = total + (across + pltpu.roll(across, 1 if yp == 0 else self.rows - 1, 0))
                total = total + (S[c, yp, xp, zi - 1] + S[c, yp, xp, zi + 1])
                local.append(stiff * total + K[2 * sweep + c, yp, xp, zi])
            square = local[0] * local[0] + local[1] * local[1]
            scale = lax.rsqrt(1.0 + square)
            for c in (0, 1):
                S[c, yp, xp, zi] = local[c] * scale
            if 0 <= z < self.depth:
                energy = (square * scale)[: self.half]
                acc = acc + sum(energy[8 * j : 8 * j + 8] for j in range(self.half // 8))
        return acc


def inner_planes(depth, t):
    phase = t // 4
    return range(2 + phase, depth - 1 - phase, 2)


def outer_planes(depth, t):
    phase = t // 4
    reach = 2 * (SWEEPS - 1 - t // 8)
    parity = phase % 2
    return [z for z in range(parity - reach, depth - parity + reach + 1, 2) if z not in inner_planes(depth, t)]


def build_kernel(*refs):
    own, other = refs[:3], refs[3:6]
    S, ST, K = refs[6:]
    depth, height, _ = own[2].shape
    rows = Rows(S, ST, K, depth, height)

    def two(p, carry):
        for field in ALL:
            for z in (2 * p, 2 * p + 1):
                for y in (0, 1):
                    a, b = (load_field(*side, field, z, pl.ds(y, height // 2, stride=2)) for side in (own, other))
                    rows.put(field, z + 3, y, 0, a, b)
        return carry

    lax.fori_loop(0, depth // 2, two, 0)


def build(own, other):
    depth, height, lanes = own[2].shape
    rows = -(-(height // 2 + 4) // 8) * 8
    planes = depth + 7
    return pl.pallas_call(
        build_kernel,
        out_shape=[
            jax.ShapeDtypeStruct((2, 2, 2, planes, rows, lanes), F32),
            jax.ShapeDtypeStruct((2, 2, planes, rows, lanes), F32),
            jax.ShapeDtypeStruct((2 * SWEEPS, 2, 2, planes, rows, lanes), F32),
        ],
        in_specs=[VMEM] * 6,
        out_specs=[VMEM] * 3,
        compiler_params=pltpu.CompilerParams(vmem_limit_bytes=8 << 20),
        cost_estimate=pl.CostEstimate(flops=30_000_000, bytes_accessed=10_000_000, transcendentals=0),
        name="build",
    )(*own, *other)


def middle_kernel(*refs):
    sides = refs[3:5]
    height = 2 * refs[5][0]
    S, ST, K, E = refs[6:]
    depth = S.shape[3] - 7
    rows = Rows(S, ST, K, depth, height)
    high = 5 * depth // 4

    def four(q, carry):
        for field in ALL:
            source = field if field in FIRST else field - 5
            for j in range(4):
                for y in (0, 1):
                    a, b = (
                        rows.rows_beyond(
                            side[high + source * (depth // 2) + 2 * q + j // 2],
                            side[source * (depth // 4) + q],
                            j,
                            y,
                            field not in FIRST,
                        )
                        for side in sides
                    )
                    rows.put(field, 4 * q + j + 3, y, height // 2, a, b)
        return carry

    lax.fori_loop(0, depth // 4, four, 0)
    for t in range(8 * SWEEPS):
        E[t] = rows.section(t, inner_planes(depth, t))


def middle(state, own, other, height):
    lanes = own.shape[-1]

    def kernel(*refs):
        middle_kernel(*refs[:5], (height // 2,), *refs[5:])

    return pl.pallas_call(
        kernel,
        out_shape=[jax.ShapeDtypeStruct(v.shape, F32) for v in state] + [jax.ShapeDtypeStruct((8 * SWEEPS, 8, lanes), F32)],
        in_specs=[VMEM] * 5,
        out_specs=[VMEM] * 4,
        input_output_aliases={0: 0, 1: 1, 2: 2},
        compiler_params=pltpu.CompilerParams(vmem_limit_bytes=8 << 20),
        cost_estimate=pl.CostEstimate(flops=30_000_000, bytes_accessed=10_000_000, transcendentals=0),
        name="middle",
    )(*state, own, other)


def last_kernel(*refs):
    E = refs[3]
    own, other = refs[4:7], refs[7:10]
    S, ST, K, out, energies, lines, final, sems = refs[10:]
    depth, height, lanes = out.shape[1:]
    rows = Rows(S, ST, K, depth, height)
    sides = (own, other)
    for c in range(2):
        for y in range(2):
            for x in range(2):
                S[c, y, x, 0] = jnp.zeros((rows.rows, lanes), F32)
                S[c, y, x, depth + 6] = jnp.zeros((rows.rows, lanes), F32)
    for which, listed, base, names in ((0, up_planes(depth), -depth, ("cuu", "cud")), (1, down_planes(), depth, ("cdu", "cdd"))):
        for n, (field, z) in enumerate(listed):
            for y in (0, 1):
                a, b = (
                    jnp.concatenate(
                        [
                            side[which][n, pl.ds(y, height // 2, stride=2), :],
                            rows.corner(side[2], names, n, y),
                        ],
                        axis=0,
                    )
                    for side in sides
                )
                rows.put(field, z + base + 3, y, 0, a, b)
    half = height // 2
    sent = []

    def send(start, stop):
        for z in range(start, stop):
            for c in (0, 1):
                for y in (0, 1):
                    value = jnp.where(rows.even[:half], S[c, y, 0, z + 3, :half], S[c, y, 1, z + 3, :half])
                    final[c, z, pl.ds(y, half, stride=2), :] = value
        part = pl.ds(start, stop - start)
        copy = pltpu.make_async_copy(final.at[:, part], out.at[:, part], sems.at[len(sent)])
        copy.start()
        sent.append(copy)

    low, high = 2 * SWEEPS, depth - 2 * SWEEPS + 1
    send(low, high)
    for t in range(8 * SWEEPS):
        acc = E[t] + rows.section(t, outer_planes(depth, t))
        mine = rows.lane % 2 == t % 2
        lines[pl.ds(t, 1), :] = jnp.sum(jnp.where(mine, acc, 0.0), axis=0, keepdims=True)

    send(0, low)
    send(high, depth)
    total = jnp.sum(lines[...], axis=1, keepdims=True)
    diagonal = lax.broadcasted_iota(jnp.int32, lines.shape, 0) == lax.broadcasted_iota(jnp.int32, lines.shape, 1)
    line = jnp.sum(jnp.where(diagonal, total, 0.0), axis=0, keepdims=True)
    energies[...] = jnp.broadcast_to(line, energies.shape)
    for copy in sent:
        copy.wait()


def last(state, own, other, shape, devices):
    lanes = shape[-1]
    results = pl.pallas_call(
        last_kernel,
        out_shape=[jax.ShapeDtypeStruct(v.shape, F32) for v in state[:3]]
        + [jax.ShapeDtypeStruct(shape, F32), jax.ShapeDtypeStruct((devices, lanes), F32)],
        in_specs=[VMEM] * 10,
        out_specs=[VMEM] * 3 + [pl.BlockSpec(memory_space=pltpu.HBM), VMEM],
        input_output_aliases={0: 0, 1: 1, 2: 2},
        scratch_shapes=[
            pltpu.VMEM((8 * SWEEPS, lanes), F32),
            pltpu.VMEM(shape, F32),
            pltpu.SemaphoreType.DMA((3,)),
        ],
        compiler_params=pltpu.CompilerParams(vmem_limit_bytes=8 << 20),
        cost_estimate=pl.CostEstimate(flops=30_000_000, bytes_accessed=10_000_000, transcendentals=0),
        name="last",
    )(*state, *own, *other)
    return results[3:]


def step(spins, kicks, stiffness):
    nz, ny, nx = (lax.axis_size(a) for a in ("gz", "gy", "gx"))
    devices = nz * ny * nx
    sites = jnp.float32(stiffness.size * devices // 8)

    def shift(value, even_core, odd_core):
        pairs = []
        for z in range(nz):
            for y in range(ny):
                for x in range(nx):
                    dz, dy = odd_core if x % 2 else even_core
                    pairs.append(((z * ny + y) * nx + x, ((z + dz) % nz * ny + (y + dy) % ny) * nx + x))
        return lax.ppermute(value, ("gz", "gy", "gx"), pairs)

    def swap(value):
        return lax.ppermute(value, "gx", [(i, i ^ 1) for i in range(nx)])

    lanes = stiffness.shape[-1]

    def beside(value):
        right = lax.ppermute(value, "gx", [((i + 1) % nx, i) for i in range(nx)])
        if nx == 2:
            return right
        left = lax.ppermute(value, "gx", [(i, (i + 1) % nx) for i in range(nx)])
        lane = lax.broadcasted_iota(jnp.int32, value.shape, value.ndim - 1)
        return jnp.where(lane < lanes // 2, right, left)

    raw = (spins, kicks, stiffness)
    zup, zdn = pack_faces(*raw)
    yup, ydn, mine = pack_edges(*raw, zup, zdn)
    first, second = share_out(lanes, mine, swap(mine))
    up, down, left, right = (1, 0), (-1, 0), (0, -1), (0, 1)
    zlo, zhi = shift(zup, up, up), shift(zdn, down, down)
    edges = join(shift(yup, right, right), shift(ydn, left, left))
    corners = stack_corners(lanes, shift(first, (-1, -1), (-1, 1)), shift(second, (1, -1), (1, 1)))
    beyond = beside(edges)
    other = tuple(beside(v) for v in raw)
    state = build(raw, other)
    state = middle(state, edges, beyond, stiffness.shape[1])
    corners, beyond = sort_corners(lanes, corners, swap(corners))
    if nx > 2:
        beyond = beside(corners)
    other = (beside(zlo), beside(zhi), beyond)
    final, energies = last(state, (zlo, zhi, corners), other, spins.shape, devices)
    parts = lax.all_to_all(energies, ("gz", "gy", "gx"), 0, 0, tiled=True)
    total = jnp.sum(parts, axis=0)[: 8 * SWEEPS]
    return (final, -total / sites)


def solution(mesh):
    placed = (P(None, "gz", "gy", "gx"), P(None, None, "gz", "gy", "gx"), P("gz", "gy", "gx"))
    return jax.shard_map(
        step,
        mesh=mesh,
        in_specs=placed,
        out_specs=(P(None, "gz", "gy", "gx"), P()),
        check_vma=False,
    )
```

profile of v0, /device:TPU:0, one launch (start us, length us, event | category | flops | bytes accessed | tf_op | source)
XLA Modules:
  0.0 59.3 jit_solution(7153919057934126220)
XLA Ops:
  0.7 0.6 collective-permute-start.1
  1.2 2.3 %faces.1 = (f32[10,48,128]{2,1,0:T(8,128)S(1)}, f32[17,48,128]{2,1,0:T(8,128)}) custom-call(f32[2,16,48,128]{3,2,1,0:T(8,128)} %s_ref.3, f32[2,2,16,48,128]{4,3,2,1,0:T(8,128)} %k_ref.3, f32[16,48,128]{2,1,0:T(8,128)} %st_ref.3), custom_call_target="tpu_custom_call" | custom-call | flops 1000000 | bytes 1000000 | tf_op jit(solution)/shard_map/faces/pallas_call | solution.py:147
  3.5 3.4 %collective-permute-start.7 = (f32[17,48,128]{2,1,0:T(8,128)}, f32[17,48,128]{2,1,0:T(8,128)S(1)}, u32[]{:S(2)}, u32[]{:S(2)}) collective-permute-start(f32[17,48,128]{2,1,0:T(8,128)} %get-tuple-element.24.zdn), channel_id=1, source_target_pairs={{0,24},{1,25},{2,26},{3,27},{4,28},{5,29},{6,30},{7,31},{8,0},{9,1... | collective-permute-start | bytes 1253384 | tf_op jit(solution)/shard_map/ppermute | solution.py:511
  6.9 1.0 %copy-done.3 = f32[17,48,128]{2,1,0:T(8,128)S(1)} copy-done((f32[17,48,128]{2,1,0:T(8,128)S(1)}, f32[17,48,128]{2,1,0:T(8,128)}, u32[]{:S(2)}) %copy-start.3) | copy-done | bytes 417816
  8.0 0.2 edges.1
  8.2 0.2 collective-permute-start.8
  8.4 0.4 collective-permute-start
  8.8 0.7 %collective-permute-done.8.pair = f32[11,8,128]{2,1,0:T(8,128)S(1)} collective-permute-done((f32[11,8,128]{2,1,0:T(8,128)S(1)}, f32[11,8,128]{2,1,0:T(8,128)S(1)}, u32[]{:S(2)}, u32[]{:S(2)}) %collective-permute-start.8) | collective-permute-done | bytes 45088 | tf_op jit(solution)/shard_map/ppermute | solution.py:514
  9.5 2.6 %collective-permute-start.10 = (f32[4,8,128]{2,1,0:T(8,128)S(1)}, f32[4,8,128]{2,1,0:T(8,128)S(1)}, u32[]{:S(2)}, u32[]{:S(2)}) collective-permute-start(f32[4,8,128]{2,1,0:T(8,128)S(1)} %get-tuple-element.33), channel_id=1, source_target_pairs={{0,14},{1,11},{2,8},{3,13},{4,10},{5,15},{6,12},{7,9},{8,22},{9,19... | collective-permute-start | bytes 49160 | tf_op jit(solution)/shard_map/ppermute | solution.py:511
  12.1 0.0 collective-permute-start.3
  12.1 3.0 %collective-permute-done.10.second = f32[4,8,128]{2,1,0:T(8,128)S(1)} collective-permute-done((f32[4,8,128]{2,1,0:T(8,128)S(1)}, f32[4,8,128]{2,1,0:T(8,128)S(1)}, u32[]{:S(2)}, u32[]{:S(2)}) %collective-permute-start.10) | collective-permute-done | bytes 16416 | tf_op jit(solution)/shard_map/ppermute | solution.py:511
  15.1 4.5 %collective-permute-start.9 = (f32[10,8,128]{2,1,0:T(8,128)S(1)}, f32[10,8,128]{2,1,0:T(8,128)S(1)}, u32[]{:S(2)}, u32[]{:S(2)}) collective-permute-start(f32[10,8,128]{2,1,0:T(8,128)S(1)} %get-tuple-element.32), channel_id=1, source_target_pairs={{0,30},{1,27},{2,24},{3,29},{4,26},{5,31},{6,28},{7,25},{8,6},{9,3... | collective-permute-start | bytes 122888 | tf_op jit(solution)/shard_map/ppermute | solution.py:511
  19.6 1.7 %collective-permute-done.9.first = f32[10,8,128]{2,1,0:T(8,128)S(1)} collective-permute-done((f32[10,8,128]{2,1,0:T(8,128)S(1)}, f32[10,8,128]{2,1,0:T(8,128)S(1)}, u32[]{:S(2)}, u32[]{:S(2)}) %collective-permute-start.9) | collective-permute-done | bytes 40992 | tf_op jit(solution)/shard_map/ppermute | solution.py:511
  21.3 0.2 collective-permute-start.11
  21.5 0.0 collective-permute-done.3.lo
  21.5 5.8 %collective-permute-start.4 = (f32[40,8,128]{2,1,0:T(8,128)S(1)}, f32[40,8,128]{2,1,0:T(8,128)S(1)}, u32[]{:S(2)}, u32[]{:S(2)}) collective-permute-start(f32[40,8,128]{2,1,0:T(8,128)S(1)} %get-tuple-element.26), channel_id=1, source_target_pairs={{0,6},{1,7},{2,0},{3,1},{4,2},{5,3},{6,4},{7,5},{8,14},{9,15},{10,... | collective-permute-start | bytes 491528 | tf_op jit(solution)/shard_map/ppermute | solution.py:511
  27.3 0.0 collective-permute-done.11.pair
  27.3 0.2 collective-permute-start.2
  27.5 3.9 %collective-permute-done.4.hi = f32[40,8,128]{2,1,0:T(8,128)S(1)} collective-permute-done((f32[40,8,128]{2,1,0:T(8,128)S(1)}, f32[40,8,128]{2,1,0:T(8,128)S(1)}, u32[]{:S(2)}, u32[]{:S(2)}) %collective-permute-start.4) | collective-permute-done | bytes 163872 | tf_op jit(solution)/shard_map/ppermute | solution.py:511
  31.4 8.3 %collective-permute-done.6.refs_4_ = f32[10,48,128]{2,1,0:T(8,128)S(1)} collective-permute-done((f32[10,48,128]{2,1,0:T(8,128)S(1)}, f32[10,48,128]{2,1,0:T(8,128)S(1)}, u32[]{:S(2)}, u32[]{:S(2)}) %collective-permute-start.6) | collective-permute-done | bytes 245792 | tf_op jit(solution)/shard_map/ppermute | solution.py:511
  39.7 0.0 collective-permute-start.5
  39.7 0.0 collective-permute-done.2.refs_5_
  39.7 0.5 collective-permute-start.12
  40.2 0.0 collective-permute-done.refs_3_
  40.2 0.0 collective-permute-done.1.refs_4_
  40.3 1.2 %build.1 = (f32[2,2,2,23,32,128]{5,4,3,2,1,0:T(8,128)S(1)}, f32[2,2,23,32,128]{4,3,2,1,0:T(8,128)S(1)}, f32[4,2,2,23,32,128]{5,4,3,2,1,0:T(8,128)S(1)}) custom-call(f32[2,16,48,128]{3,2,1,0:T(8,128)S(1)} %copy-done.1, f32[2,2,16,48,128]{4,3,2,1,0:T(8,128)S(1)} %copy-done, f32[16,48,128]{2,1,0:T(8,128)S(1)} %copy-done.2, ...), custom_call_target="tpu_custom_call" | custom-call | flops 30000000 | bytes 10000000 | tf_op jit(solution)/shard_map/build/pallas_call | solution.py:357
  41.5 2.8 %middle.1 = (f32[2,2,2,23,32,128]{5,4,3,2,1,0:T(8,128)S(1)}, f32[2,2,23,32,128]{4,3,2,1,0:T(8,128)S(1)}, f32[4,2,2,23,32,128]{5,4,3,2,1,0:T(8,128)S(1)}, f32[16,8,128]{2,1,0:T(8,128)S(1)}) custom-call(f32[2,2,2,23,32,128]{5,4,3,2,1,0:T(8,128)S(1)} %get-tuple-element.20.refs_0_, ...), custom_call_target="tpu_custom_call", output_to_operand_aliasing={{0}: (0, {}), {1}: (1, {}), {2}: (2, {})} | custom-call | flops 30000000 | bytes 10000000 | tf_op jit(solution)/shard_map/middle/pallas_call | solution.py:409
  44.3 0.0 collective-permute-done.12.refs_7_
  44.3 2.8 %last.1 = (f32[2,2,2,23,32,128]{5,4,3,2,1,0:T(8,128)S(1)}, f32[2,2,23,32,128]{4,3,2,1,0:T(8,128)S(1)}, f32[4,2,2,23,32,128]{5,4,3,2,1,0:T(8,128)S(1)}, f32[2,16,48,128]{3,2,1,0:T(8,128)}, f32[32,128]{1,0:T(8,128)S(1)}) custom-call(f32[2,2,2,23,32,128]{5,4,3,2,1,0:T(8,128)S(1)} %get-tuple-element.27.refs_0_, ...), custom_call_target="tpu_custom_call", output_to_operand_aliasing={{0}: (0, {}), {1}: (1, {}), {2}: (2, {})} | custom-call | flops 30000000 | bytes 10000000 | tf_op jit(solution)/shard_map/last/pallas_call | solution.py:480
  47.1 11.6 %all_to_all.9 = f32[32,1,128]{2,1,0:T(1,128)S(1)} all-to-all(f32[32,1,128]{2,1,0:T(1,128)S(1)} %bitcast.3), channel_id=1, replica_groups=mesh['gz'=4,'gy'=4,'gx'=2] {'gz','gy','gx'}, dimensions={0} | all-to-all | bytes 32768 | tf_op jit(solution)/shard_map/all_to_all | solution.py:543
  58.7 0.1 reduce_sum.9
  58.8 0.5 negate_multiply_fusion
  (16 shorter events, 0.1 us)
Async XLA Ops:
  0.6 6.3 %copy-start = (f32[2,2,16,48,128]{4,3,2,1,0:T(8,128)S(1)}, f32[2,2,16,48,128]{4,3,2,1,0:T(8,128)}, u32[]{:S(2)}) copy-start(f32[2,2,16,48,128]{4,3,2,1,0:T(8,128)} %k_ref.3) | copy-start | bytes 4718596
  0.6 6.3 %copy-start.2 = (f32[16,48,128]{2,1,0:T(8,128)S(1)}, f32[16,48,128]{2,1,0:T(8,128)}, u32[]{:S(2)}) copy-start(f32[16,48,128]{2,1,0:T(8,128)} %st_ref.3) | copy-start | bytes 1179652
  0.6 6.3 %copy-start.1 = (f32[2,16,48,128]{3,2,1,0:T(8,128)S(1)}, f32[2,16,48,128]{3,2,1,0:T(8,128)}, u32[]{:S(2)}) copy-start(f32[2,16,48,128]{3,2,1,0:T(8,128)} %s_ref.3) | copy-start | bytes 2359300
  0.7 39.6 %collective-permute-start.1 = (f32[2,2,16,48,128]{4,3,2,1,0:T(8,128)}, f32[2,2,16,48,128]{4,3,2,1,0:T(8,128)S(1)}, u32[]{:S(2)}, u32[]{:S(2)}) collective-permute-start(f32[2,2,16,48,128]{4,3,2,1,0:T(8,128)} %k_ref.3), channel_id=1, source_target_pairs={{1,0},{0,1},{3,2},{2,3},{5,4},{4,5},{7,6},{6,7},{9,8},{8,9},{11,10... | collective-permute-start | bytes 4718600 | tf_op jit(solution)/shard_map/ppermute | solution.py:519
  3.5 27.9 %collective-permute-start.7 = (f32[17,48,128]{2,1,0:T(8,128)}, f32[17,48,128]{2,1,0:T(8,128)S(1)}, u32[]{:S(2)}, u32[]{:S(2)}) collective-permute-start(f32[17,48,128]{2,1,0:T(8,128)} %get-tuple-element.24.zdn), channel_id=1, source_target_pairs={{0,24},{1,25},{2,26},{3,27},{4,28},{5,29},{6,30},{7,31},{8,0},{9,1... | collective-permute-start | bytes 1253384 | tf_op jit(solution)/shard_map/ppermute | solution.py:511
  6.9 1.0 %copy-start.3 = (f32[17,48,128]{2,1,0:T(8,128)S(1)}, f32[17,48,128]{2,1,0:T(8,128)}, u32[]{:S(2)}) copy-start(f32[17,48,128]{2,1,0:T(8,128)} %get-tuple-element.24.zdn) | copy-start | bytes 1253380
  8.2 1.3 %collective-permute-start.8 = (f32[11,8,128]{2,1,0:T(8,128)S(1)}, f32[11,8,128]{2,1,0:T(8,128)S(1)}, u32[]{:S(2)}, u32[]{:S(2)}) collective-permute-start(f32[11,8,128]{2,1,0:T(8,128)S(1)} %get-tuple-element.31.mine), channel_id=1, source_target_pairs={{0,1},{1,0},{2,3},{3,2},{4,5},{5,4},{6,7},{7,6},{8,9},{9,8},{10,11... | collective-permute-start | bytes 135176 | tf_op jit(solution)/shard_map/ppermute | solution.py:514
  8.4 31.9 %collective-permute-start = (f32[2,16,48,128]{3,2,1,0:T(8,128)S(1)}, f32[2,16,48,128]{3,2,1,0:T(8,128)S(1)}, u32[]{:S(2)}, u32[]{:S(2)}) collective-permute-start(f32[2,16,48,128]{3,2,1,0:T(8,128)S(1)} %copy-done.1), channel_id=1, source_target_pairs={{1,0},{0,1},{3,2},{2,3},{5,4},{4,5},{7,6},{6,7},{9,8},{8,9},{11,10... | collective-permute-start | bytes 2359304 | tf_op jit(solution)/shard_map/ppermute | solution.py:519
  9.5 5.6 %collective-permute-start.10 = (f32[4,8,128]{2,1,0:T(8,128)S(1)}, f32[4,8,128]{2,1,0:T(8,128)S(1)}, u32[]{:S(2)}, u32[]{:S(2)}) collective-permute-start(f32[4,8,128]{2,1,0:T(8,128)S(1)} %get-tuple-element.33), channel_id=1, source_target_pairs={{0,14},{1,11},{2,8},{3,13},{4,10},{5,15},{6,12},{7,9},{8,22},{9,19... | collective-permute-start | bytes 49160 | tf_op jit(solution)/shard_map/ppermute | solution.py:511
  12.1 9.4 %collective-permute-start.3 = (f32[20,8,128]{2,1,0:T(8,128)S(1)}, f32[20,8,128]{2,1,0:T(8,128)S(1)}, u32[]{:S(2)}, u32[]{:S(2)}) collective-permute-start(f32[20,8,128]{2,1,0:T(8,128)S(1)} %get-tuple-element.25), channel_id=1, source_target_pairs={{0,2},{1,3},{2,4},{3,5},{4,6},{5,7},{6,0},{7,1},{8,10},{9,11},{10,... | collective-permute-start | bytes 245768 | tf_op jit(solution)/shard_map/ppermute | solution.py:511
  15.1 6.2 %collective-permute-start.9 = (f32[10,8,128]{2,1,0:T(8,128)S(1)}, f32[10,8,128]{2,1,0:T(8,128)S(1)}, u32[]{:S(2)}, u32[]{:S(2)}) collective-permute-start(f32[10,8,128]{2,1,0:T(8,128)S(1)} %get-tuple-element.32), channel_id=1, source_target_pairs={{0,30},{1,27},{2,24},{3,29},{4,26},{5,31},{6,28},{7,25},{8,6},{9,3... | collective-permute-start | bytes 122888 | tf_op jit(solution)/shard_map/ppermute | solution.py:511
  21.3 6.0 %collective-permute-start.11 = (f32[14,8,128]{2,1,0:T(8,128)S(1)}, f32[14,8,128]{2,1,0:T(8,128)S(1)}, u32[]{:S(2)}, u32[]{:S(2)}) collective-permute-start(f32[14,8,128]{2,1,0:T(8,128)S(1)} %shard_map.52.got), channel_id=1, source_target_pairs={{0,1},{1,0},{2,3},{3,2},{4,5},{5,4},{6,7},{7,6},{8,9},{9,8},{10,11... | collective-permute-start | bytes 172040 | tf_op jit(solution)/shard_map/ppermute | solution.py:514
  21.5 9.8 %collective-permute-start.4 = (f32[40,8,128]{2,1,0:T(8,128)S(1)}, f32[40,8,128]{2,1,0:T(8,128)S(1)}, u32[]{:S(2)}, u32[]{:S(2)}) collective-permute-start(f32[40,8,128]{2,1,0:T(8,128)S(1)} %get-tuple-element.26), channel_id=1, source_target_pairs={{0,6},{1,7},{2,0},{3,1},{4,2},{5,3},{6,4},{7,5},{8,14},{9,15},{10,... | collective-permute-start | bytes 491528 | tf_op jit(solution)/shard_map/ppermute | solution.py:511
  27.3 12.4 %collective-permute-start.2 = (f32[16,48,128]{2,1,0:T(8,128)S(1)}, f32[16,48,128]{2,1,0:T(8,128)S(1)}, u32[]{:S(2)}, u32[]{:S(2)}) collective-permute-start(f32[16,48,128]{2,1,0:T(8,128)S(1)} %copy-done.2), channel_id=1, source_target_pairs={{1,0},{0,1},{3,2},{2,3},{5,4},{4,5},{7,6},{6,7},{9,8},{8,9},{11,10... | collective-permute-start | bytes 1179656 | tf_op jit(solution)/shard_map/ppermute | solution.py:519
  31.4 8.3 %collective-permute-start.6 = (f32[10,48,128]{2,1,0:T(8,128)S(1)}, f32[10,48,128]{2,1,0:T(8,128)S(1)}, u32[]{:S(2)}, u32[]{:S(2)}) collective-permute-start(f32[10,48,128]{2,1,0:T(8,128)S(1)} %get-tuple-element.23.zup), channel_id=1, source_target_pairs={{0,8},{1,9},{2,10},{3,11},{4,12},{5,13},{6,14},{7,15},{8,16},{9,17... | collective-permute-start | bytes 737288 | tf_op jit(solution)/shard_map/ppermute | solution.py:511
  31.4 12.9 %collective-permute-start.13 = (f32[17,48,128]{2,1,0:T(8,128)S(1)}, f32[17,48,128]{2,1,0:T(8,128)S(1)}, u32[]{:S(2)}, u32[]{:S(2)}) collective-permute-start(f32[17,48,128]{2,1,0:T(8,128)S(1)} %collective-permute-done.7.refs_5_), channel_id=1, source_target_pairs={{1,0},{0,1},{3,2},{2,3},{5,4},{4,5},{7,6},{6,7},{9,8},{8,9},{11,10... | collective-permute-start | bytes 1253384 | tf_op jit(solution)/shard_map/ppermute | solution.py:519
  39.7 1.8 %collective-permute-start.5 = (f32[60,8,128]{2,1,0:T(8,128)S(1)}, f32[60,8,128]{2,1,0:T(8,128)S(1)}, u32[]{:S(2)}, u32[]{:S(2)}) collective-permute-start(f32[60,8,128]{2,1,0:T(8,128)S(1)} %shard_map.50.refs_3_), channel_id=1, source_target_pairs={{1,0},{0,1},{3,2},{2,3},{5,4},{4,5},{7,6},{6,7},{9,8},{8,9},{11,10... | collective-permute-start | bytes 737288 | tf_op jit(solution)/shard_map/ppermute | solution.py:519
  39.7 4.6 %collective-permute-start.12 = (f32[10,48,128]{2,1,0:T(8,128)S(1)}, f32[10,48,128]{2,1,0:T(8,128)S(1)}, u32[]{:S(2)}, u32[]{:S(2)}) collective-permute-start(f32[10,48,128]{2,1,0:T(8,128)S(1)} %collective-permute-done.6.refs_4_), channel_id=1, source_target_pairs={{1,0},{0,1},{3,2},{2,3},{5,4},{4,5},{7,6},{6,7},{9,8},{8,9},{11,10... | collective-permute-start | bytes 737288 | tf_op jit(solution)/shard_map/ppermute | solution.py:519
where the time goes:
time: 59.5 us; the launch traced here: 59.3 us
  starting transfers between devices  18.3 us (31%)
  waiting for transfers between devices  17.6 us (30%)
  blocking collectives  11.6 us (19%)
  Pallas kernels  9.32 us (16%)
  local copies, waits for them, and re-layouts  1.04 us (2%)
  between operations  0.76 us (1%)
    ppermute x6, waiting for transfers between devices, shift(): return lax.ppermute(value, ('gz', 'gy', 'gx'), pairs)  16.9 us
    ppermute x6, starting transfers between devices, shift(): return lax.ppermute(value, ('gz', 'gy', 'gx'), pairs)  16.3 us
    all_to_all x1, blocking collectives, step(): parts = lax.all_to_all(energies, ('gz', 'gy', 'gx'), 0, 0, tiled=True)  11.6 us
    pallas_call x1, Pallas kernels, middle(): pl.pallas_call(kernel, out_shape=[jax.ShapeDtypeStruct(v.shape, F32) for...  2.77 us
    pallas_call x1, Pallas kernels, last(): pl.pallas_call(last_kernel, out_shape=[jax.ShapeDtypeStruct(v.shape, F32)...  2.76 us
    pallas_call x1, Pallas kernels, pack_faces(): pl.pallas_call(face_kernel, out_shape=[jax.ShapeDtypeStruct((n, height, l...  2.29 us
    ppermute x6, starting transfers between devices, beside(): right = lax.ppermute(value, 'gx', [((i + 1) % nx, i) for i in range(nx)])  1.62 us
    pallas_call x1, Pallas kernels, build(): pl.pallas_call(build_kernel, out_shape=[jax.ShapeDtypeStruct((2, 2, 2, pl...  1.25 us
  transfers between devices with their start and end apart: 14, of which 5 were waited for; matrix products, arithmetic and copies ran while one was open for 0% of the time, Pallas kernels for 11%

commit v1 on v0

--- a/solution.py
+++ b/solution.py
@@ -44,6 +44,25 @@
     return listed + [(n, r) for n in (15, 16) for r in second]
 
 
+def place_of(planes, n, height):
+    short = [m for m, (f, z) in enumerate(planes) if f < 2 and z % 2 == 0]
+    whole = [m for m in range(len(planes)) if m not in short]
+    half = height // 2
+    packed = half + packed_even(half)
+    if n in short:
+        return len(whole) * height + short.index(n) * packed, True
+    return whole.index(n) * height, False
+
+
+def packed_even(half):
+    return -(-half // 16) * 8
+
+
+def face_rows(planes, height):
+    short = sum(f < 2 and z % 2 == 0 for f, z in planes)
+    return (len(planes) - short) * height + short * (height // 2 + packed_even(height // 2))
+
+
 def load_field(s_ref, k_ref, st_ref, field, z, rows=slice(None)):
     return field_ref(s_ref, k_ref, st_ref, field)[z, rows, :]
 
@@ -64,20 +83,34 @@
         c.wait()
 
 
-def face_kernel(s_ref, k_ref, st_ref, zup, zdn, far, sems):
-    depth, _, _ = st_ref.shape
+def face_kernel(s_ref, k_ref, st_ref, zup, zdn, far, raw, sems):
+    depth, height, lanes = st_ref.shape
+    half = height // 2
+    keep = packed_even(half)
     get = functools.partial(field_ref, s_ref, k_ref, st_ref)
     moves = [(s_ref.at[:, depth - 3], far.at[0]), (s_ref.at[:, 3], far.at[1])]
-    for f in FIRST:
-        moves.append((get(f).at[pl.ds(0, 3)], zdn.at[pl.ds(3 * f, 3)]))
-        moves.append((get(f).at[pl.ds(depth - 2, 2)], zup.at[pl.ds(2 * f, 2)]))
-    moves += [(get(5).at[pl.ds(0, 1)], zdn.at[pl.ds(15, 1)]), (get(6).at[pl.ds(0, 1)], zdn.at[pl.ds(16, 1)])]
+    packed = []
+    for out, planes in ((zup, up_planes(depth)), (zdn, down_planes())):
+        for n, (f, z) in enumerate(planes):
+            start, short = place_of(planes, n, height)
+            if short:
+                moves.append((get(f).at[z], raw.at[len(packed)]))
+                packed.append((out, start))
+            else:
+                moves.append((get(f).at[z], out.at[pl.ds(start, height)]))
     copy_all(moves, sems)
-    for c in (0, 1):
-        n = 2 * (3 + c)
-        zup[n] = zup[n] + zup[4] * far[0, c]
-        n = 3 * (3 + c) + 2
-        zdn[n] = zdn[n] + zdn[8] * far[1, c]
+    even = lax.broadcasted_iota(jnp.int32, (half - keep, lanes), 1) % 2 == 0
+    for m, (out, start) in enumerate(packed):
+        rows = raw[m, pl.ds(0, half, stride=2), :]
+        rest = pltpu.roll(rows[keep:], lanes - 1, 1)
+        out[start : start + half] = raw[m, pl.ds(1, half, stride=2), :]
+        out[start + half : start + half + half - keep] = jnp.where(even, rest, rows[: half - keep])
+        out[start + 2 * half - keep : start + half + keep] = rows[half - keep : keep]
+    for out, planes, z, side in ((zup, up_planes(depth), depth - 2, 0), (zdn, down_planes(), 2, 1)):
+        stiff, _ = place_of(planes, planes.index((2, z)), height)
+        for c in (0, 1):
+            start, _ = place_of(planes, planes.index((3 + c, z)), height)
+            out[start : start + height] = out[start : start + height] + out[stiff : stiff + height] * far[side, c]
 
 
 def edge_kernel(s_ref, k_ref, st_ref, zup, zdn, up, down, corners, s_low, s_high, k_low, k_high, t_low, t_high, sems):
@@ -105,10 +138,17 @@
         return jnp.where(lower, a, b)
 
     for name, (start, count) in CORNERS.items():
-        src = zup if name[1] == "u" else zdn
+        src, planes = (zup, up_planes(depth)) if name[1] == "u" else (zdn, down_planes())
         tiles = [jnp.zeros((8, lanes), F32)] * count
         for i, (n, r) in enumerate(corner_rows(name)):
-            value, place = (src[n, first, :], r) if r >= 0 else (src[n, last, :], 8 + r)
+            place = r if r >= 0 else 8 + r
+            field, z = planes[n]
+            if field < 2:
+                value = s_low[field, z] if r >= 0 else s_high[field, z]
+            else:
+                base, _ = place_of(planes, n, height)
+                base = base if r >= 0 else base + height - 8
+                value = src[base : base + 8]
             shift = (i - place) % 8
             value = pltpu.roll(value, shift, 0) if shift else value
             tiles[i // 8] = jnp.where(sub == i % 8, value, tiles[i // 8])
@@ -143,13 +183,18 @@
 
 
 def pack_faces(spins, kicks, stiffness):
-    _, height, lanes = stiffness.shape
+    depth, height, lanes = stiffness.shape
+    lists = (up_planes(depth), down_planes())
     return pl.pallas_call(
         face_kernel,
-        out_shape=[jax.ShapeDtypeStruct((n, height, lanes), F32) for n in (10, 17)],
+        out_shape=[jax.ShapeDtypeStruct((face_rows(p, height), lanes), F32) for p in lists],
         in_specs=[pl.BlockSpec(memory_space=pltpu.HBM)] * 3,
         out_specs=[VMEM] * 2,
-        scratch_shapes=[pltpu.VMEM((2, 2, height, lanes), F32), pltpu.SemaphoreType.DMA((14,))],
+        scratch_shapes=[
+            pltpu.VMEM((2, 2, height, lanes), F32),
+            pltpu.VMEM((6, height, lanes), F32),
+            pltpu.SemaphoreType.DMA((29,)),
+        ],
         compiler_params=pltpu.CompilerParams(vmem_limit_bytes=FACE_GRANT),
         cost_estimate=pl.CostEstimate(flops=1_000_000, bytes_accessed=1_000_000, transcendentals=0),
         name="faces",
@@ -270,6 +315,16 @@
                 self.ST[at] = value
             else:
                 self.K[(field - 3, *at)] = value
+
+    def face(self, ref, planes, n, y):
+        start, packed = place_of(planes, n, self.height)
+        if not packed:
+            return ref[pl.ds(start + y, self.half, stride=2), :]
+        if y == 1:
+            return ref[start : start + self.half]
+        keep = packed_even(self.half)
+        value = ref[start + self.half : start + self.half + keep]
+        return jnp.concatenate([value, pltpu.roll(value[: self.half - keep], 1, 1)], axis=0)
 
     def corner(self, tiles, names, n, y):
         value = jnp.zeros((8, self.lanes), F32)
@@ -436,7 +491,7 @@
                 a, b = (
                     jnp.concatenate(
                         [
-                            side[which][n, pl.ds(y, height // 2, stride=2), :],
+                            rows.face(side[which], listed, n, y),
                             rows.corner(side[2], names, n, y),
                         ],
                         axis=0,

time: 59.5 us -> 59.6 us (level)
    ppermute x2, starting transfers between devices: 0.44 us -> 1.16 us  [swap(): return lax.ppermute(value, 'gx', [(i, i ^ 1) for i in range(nx)])]
where the time goes in v1:
time: 59.6 us; the launch traced here: 59.4 us
  starting transfers between devices  18.3 us (31%)
  waiting for transfers between devices  17.6 us (30%)
  blocking collectives  11.6 us (19%)
  Pallas kernels  9.52 us (16%)
  local copies, waits for them, and re-layouts  1.01 us (2%)
  between operations  0.76 us (1%)
    ppermute x6, waiting for transfers between devices, shift(): return lax.ppermute(value, ('gz', 'gy', 'gx'), pairs)  16.7 us
    ppermute x6, starting transfers between devices, shift(): return lax.ppermute(value, ('gz', 'gy', 'gx'), pairs)  15.8 us
    all_to_all x1, blocking collectives, step(): parts = lax.all_to_all(energies, ('gz', 'gy', 'gx'), 0, 0, tiled=True)  11.6 us
    pallas_call x1, Pallas kernels, last(): pl.pallas_call(last_kernel, out_shape=[jax.ShapeDtypeStruct(v.shape, F32)...  2.9 us
    pallas_call x1, Pallas kernels, middle(): pl.pallas_call(kernel, out_shape=[jax.ShapeDtypeStruct(v.shape, F32) for...  2.77 us
    pallas_call x1, Pallas kernels, pack_faces(): pl.pallas_call(face_kernel, out_shape=[jax.ShapeDtypeStruct((face_rows(p,...  2.34 us
    ppermute x6, starting transfers between devices, beside(): right = lax.ppermute(value, 'gx', [((i + 1) % nx, i) for i in range(nx)])  1.39 us
    pallas_call x1, Pallas kernels, build(): pl.pallas_call(build_kernel, out_shape=[jax.ShapeDtypeStruct((2, 2, 2, pl...  1.25 us
  transfers between devices with their start and end apart: 14, of which 5 were waited for; matrix products, arithmetic and copies ran while one was open for 0% of the time, Pallas kernels for 11%

profile of v1, /device:TPU:0, one launch (start us, length us, event | category | flops | bytes accessed | tf_op | source)
XLA Modules:
  0.0 59.4 jit_solution(17188686561058600566)
XLA Ops:
  0.6 0.0 copy-start.1
  0.7 0.6 collective-permute-start.1
  1.2 2.3 %faces.1 = (f32[464,128]{1,0:T(8,128)S(1)}, f32[784,128]{1,0:T(8,128)}) custom-call(f32[2,16,48,128]{3,2,1,0:T(8,128)} %s_ref.3, f32[2,2,16,48,128]{4,3,2,1,0:T(8,128)} %k_ref.3, f32[16,48,128]{2,1,0:T(8,128)} %st_ref.3), custom_call_target="tpu_custom_call" | custom-call | flops 1000000 | bytes 1000000 | tf_op jit(solution)/shard_map/faces/pallas_call | solution.py:188
  3.6 3.4 %collective-permute-start.7 = (f32[784,128]{1,0:T(8,128)}, f32[784,128]{1,0:T(8,128)S(1)}, u32[]{:S(2)}, u32[]{:S(2)}) collective-permute-start(f32[784,128]{1,0:T(8,128)} %get-tuple-element.24.zdn), channel_id=1, source_target_pairs={{0,24},{1,25},{2,26},{3,27},{4,28},{5,29},{6,30},{7,31},{8,0},{9,1... | collective-permute-start | bytes 1204232 | tf_op jit(solution)/shard_map/ppermute | solution.py:566
  7.0 0.2 collective-permute-start
  7.1 1.0 %copy-done.3 = f32[784,128]{1,0:T(8,128)S(1)} copy-done((f32[784,128]{1,0:T(8,128)S(1)}, f32[784,128]{1,0:T(8,128)}, u32[]{:S(2)}) %copy-start.3) | copy-done | bytes 401432
  8.1 0.2 edges.1
  8.4 0.4 collective-permute-start.8
  8.8 0.9 %collective-permute-done.8.pair = f32[11,8,128]{2,1,0:T(8,128)S(1)} collective-permute-done((f32[11,8,128]{2,1,0:T(8,128)S(1)}, f32[11,8,128]{2,1,0:T(8,128)S(1)}, u32[]{:S(2)}, u32[]{:S(2)}) %collective-permute-start.8) | collective-permute-done | bytes 45088 | tf_op jit(solution)/shard_map/ppermute | solution.py:569
  9.7 2.6 %collective-permute-start.10 = (f32[4,8,128]{2,1,0:T(8,128)S(1)}, f32[4,8,128]{2,1,0:T(8,128)S(1)}, u32[]{:S(2)}, u32[]{:S(2)}) collective-permute-start(f32[4,8,128]{2,1,0:T(8,128)S(1)} %get-tuple-element.33), channel_id=1, source_target_pairs={{0,14},{1,11},{2,8},{3,13},{4,10},{5,15},{6,12},{7,9},{8,22},{9,19... | collective-permute-start | bytes 49160 | tf_op jit(solution)/shard_map/ppermute | solution.py:566
  12.3 0.0 collective-permute-start.3
  12.3 3.0 %collective-permute-done.10.second = f32[4,8,128]{2,1,0:T(8,128)S(1)} collective-permute-done((f32[4,8,128]{2,1,0:T(8,128)S(1)}, f32[4,8,128]{2,1,0:T(8,128)S(1)}, u32[]{:S(2)}, u32[]{:S(2)}) %collective-permute-start.10) | collective-permute-done | bytes 16416 | tf_op jit(solution)/shard_map/ppermute | solution.py:566
  15.3 4.5 %collective-permute-start.9 = (f32[10,8,128]{2,1,0:T(8,128)S(1)}, f32[10,8,128]{2,1,0:T(8,128)S(1)}, u32[]{:S(2)}, u32[]{:S(2)}) collective-permute-start(f32[10,8,128]{2,1,0:T(8,128)S(1)} %get-tuple-element.32), channel_id=1, source_target_pairs={{0,30},{1,27},{2,24},{3,29},{4,26},{5,31},{6,28},{7,25},{8,6},{9,3... | collective-permute-start | bytes 122888 | tf_op jit(solution)/shard_map/ppermute | solution.py:566
  19.8 1.7 %collective-permute-done.9.first = f32[10,8,128]{2,1,0:T(8,128)S(1)} collective-permute-done((f32[10,8,128]{2,1,0:T(8,128)S(1)}, f32[10,8,128]{2,1,0:T(8,128)S(1)}, u32[]{:S(2)}, u32[]{:S(2)}) %collective-permute-start.9) | collective-permute-done | bytes 40992 | tf_op jit(solution)/shard_map/ppermute | solution.py:566
  21.5 0.7 %collective-permute-start.11 = (f32[14,8,128]{2,1,0:T(8,128)S(1)}, f32[14,8,128]{2,1,0:T(8,128)S(1)}, u32[]{:S(2)}, u32[]{:S(2)}) collective-permute-start(f32[14,8,128]{2,1,0:T(8,128)S(1)} %shard_map.52.got), channel_id=1, source_target_pairs={{0,1},{1,0},{2,3},{3,2},{4,5},{5,4},{6,7},{7,6},{8,9},{9,8},{10,11... | collective-permute-start | bytes 172040 | tf_op jit(solution)/shard_map/ppermute | solution.py:569
  22.2 0.0 collective-permute-done.3.lo
  22.2 5.3 %collective-permute-start.4 = (f32[40,8,128]{2,1,0:T(8,128)S(1)}, f32[40,8,128]{2,1,0:T(8,128)S(1)}, u32[]{:S(2)}, u32[]{:S(2)}) collective-permute-start(f32[40,8,128]{2,1,0:T(8,128)S(1)} %get-tuple-element.26), channel_id=1, source_target_pairs={{0,6},{1,7},{2,0},{3,1},{4,2},{5,3},{6,4},{7,5},{8,14},{9,15},{10,... | collective-permute-start | bytes 491528 | tf_op jit(solution)/shard_map/ppermute | solution.py:566
  27.5 0.0 collective-permute-done.11.pair
  27.5 0.2 collective-permute-start.2
  27.7 3.9 %collective-permute-done.4.hi = f32[40,8,128]{2,1,0:T(8,128)S(1)} collective-permute-done((f32[40,8,128]{2,1,0:T(8,128)S(1)}, f32[40,8,128]{2,1,0:T(8,128)S(1)}, u32[]{:S(2)}, u32[]{:S(2)}) %collective-permute-start.4) | collective-permute-done | bytes 163872 | tf_op jit(solution)/shard_map/ppermute | solution.py:566
  31.6 0.0 collective-permute-done.7.refs_5_
  31.6 0.0 collective-permute-start.13
  31.6 8.1 %collective-permute-done.6.refs_4_ = f32[464,128]{1,0:T(8,128)S(1)} collective-permute-done((f32[464,128]{1,0:T(8,128)S(1)}, f32[464,128]{1,0:T(8,128)S(1)}, u32[]{:S(2)}, u32[]{:S(2)}) %collective-permute-start.6) | collective-permute-done | bytes 237600 | tf_op jit(solution)/shard_map/ppermute | solution.py:566
  39.7 0.0 collective-permute-start.5
  39.7 0.0 collective-permute-done.2.refs_5_
  39.7 0.5 collective-permute-start.12
  40.3 1.2 %build.1 = (f32[2,2,2,23,32,128]{5,4,3,2,1,0:T(8,128)S(1)}, f32[2,2,23,32,128]{4,3,2,1,0:T(8,128)S(1)}, f32[4,2,2,23,32,128]{5,4,3,2,1,0:T(8,128)S(1)}) custom-call(f32[2,16,48,128]{3,2,1,0:T(8,128)S(1)} %copy-done.1, f32[2,2,16,48,128]{4,3,2,1,0:T(8,128)S(1)} %copy-done, f32[16,48,128]{2,1,0:T(8,128)S(1)} %copy-done.2, ...), custom_call_target="tpu_custom_call" | custom-call | flops 30000000 | bytes 10000000 | tf_op jit(solution)/shard_map/build/pallas_call | solution.py:412
  41.5 2.8 %middle.1 = (f32[2,2,2,23,32,128]{5,4,3,2,1,0:T(8,128)S(1)}, f32[2,2,23,32,128]{4,3,2,1,0:T(8,128)S(1)}, f32[4,2,2,23,32,128]{5,4,3,2,1,0:T(8,128)S(1)}, f32[16,8,128]{2,1,0:T(8,128)S(1)}) custom-call(f32[2,2,2,23,32,128]{5,4,3,2,1,0:T(8,128)S(1)} %get-tuple-element.20.refs_0_, ...), custom_call_target="tpu_custom_call", output_to_operand_aliasing={{0}: (0, {}), {1}: (1, {}), {2}: (2, {})} | custom-call | flops 30000000 | bytes 10000000 | tf_op jit(solution)/shard_map/middle/pallas_call | solution.py:464
  44.3 2.9 %last.1 = (f32[2,2,2,23,32,128]{5,4,3,2,1,0:T(8,128)S(1)}, f32[2,2,23,32,128]{4,3,2,1,0:T(8,128)S(1)}, f32[4,2,2,23,32,128]{5,4,3,2,1,0:T(8,128)S(1)}, f32[2,16,48,128]{3,2,1,0:T(8,128)}, f32[32,128]{1,0:T(8,128)S(1)}) custom-call(f32[2,2,2,23,32,128]{5,4,3,2,1,0:T(8,128)S(1)} %get-tuple-element.27.refs_0_, ...), custom_call_target="tpu_custom_call", output_to_operand_aliasing={{0}: (0, {}), {1}: (1, {}), {2}: (2, {})} | custom-call | flops 30000000 | bytes 10000000 | tf_op jit(solution)/shard_map/last/pallas_call | solution.py:535
  47.2 11.6 %all_to_all.9 = f32[32,1,128]{2,1,0:T(1,128)S(1)} all-to-all(f32[32,1,128]{2,1,0:T(1,128)S(1)} %bitcast.3), channel_id=1, replica_groups=mesh['gz'=4,'gy'=4,'gx'=2] {'gz','gy','gx'}, dimensions={0} | all-to-all | bytes 32768 | tf_op jit(solution)/shard_map/all_to_all | solution.py:598
  58.9 0.1 reduce_sum.9
  58.9 0.5 negate_multiply_fusion
  (16 shorter events, 0.1 us)
Async XLA Ops:
  0.6 6.5 %copy-start = (f32[2,2,16,48,128]{4,3,2,1,0:T(8,128)S(1)}, f32[2,2,16,48,128]{4,3,2,1,0:T(8,128)}, u32[]{:S(2)}) copy-start(f32[2,2,16,48,128]{4,3,2,1,0:T(8,128)} %k_ref.3) | copy-start | bytes 4718596
  0.6 6.5 %copy-start.2 = (f32[16,48,128]{2,1,0:T(8,128)S(1)}, f32[16,48,128]{2,1,0:T(8,128)}, u32[]{:S(2)}) copy-start(f32[16,48,128]{2,1,0:T(8,128)} %st_ref.3) | copy-start | bytes 1179652
  0.6 6.5 %copy-start.1 = (f32[2,16,48,128]{3,2,1,0:T(8,128)S(1)}, f32[2,16,48,128]{3,2,1,0:T(8,128)}, u32[]{:S(2)}) copy-start(f32[2,16,48,128]{3,2,1,0:T(8,128)} %s_ref.3) | copy-start | bytes 2359300
  0.7 39.6 %collective-permute-start.1 = (f32[2,2,16,48,128]{4,3,2,1,0:T(8,128)}, f32[2,2,16,48,128]{4,3,2,1,0:T(8,128)S(1)}, u32[]{:S(2)}, u32[]{:S(2)}) collective-permute-start(f32[2,2,16,48,128]{4,3,2,1,0:T(8,128)} %k_ref.3), channel_id=1, source_target_pairs={{1,0},{0,1},{3,2},{2,3},{5,4},{4,5},{7,6},{6,7},{9,8},{8,9},{11,10... | collective-permute-start | bytes 4718600 | tf_op jit(solution)/shard_map/ppermute | solution.py:574
  3.6 28.0 %collective-permute-start.7 = (f32[784,128]{1,0:T(8,128)}, f32[784,128]{1,0:T(8,128)S(1)}, u32[]{:S(2)}, u32[]{:S(2)}) collective-permute-start(f32[784,128]{1,0:T(8,128)} %get-tuple-element.24.zdn), channel_id=1, source_target_pairs={{0,24},{1,25},{2,26},{3,27},{4,28},{5,29},{6,30},{7,31},{8,0},{9,1... | collective-permute-start | bytes 1204232 | tf_op jit(solution)/shard_map/ppermute | solution.py:566
  7.0 33.3 %collective-permute-start = (f32[2,16,48,128]{3,2,1,0:T(8,128)}, f32[2,16,48,128]{3,2,1,0:T(8,128)S(1)}, u32[]{:S(2)}, u32[]{:S(2)}) collective-permute-start(f32[2,16,48,128]{3,2,1,0:T(8,128)} %s_ref.3), channel_id=1, source_target_pairs={{1,0},{0,1},{3,2},{2,3},{5,4},{4,5},{7,6},{6,7},{9,8},{8,9},{11,10... | collective-permute-start | bytes 2359304 | tf_op jit(solution)/shard_map/ppermute | solution.py:574
  7.1 1.0 %copy-start.3 = (f32[784,128]{1,0:T(8,128)S(1)}, f32[784,128]{1,0:T(8,128)}, u32[]{:S(2)}) copy-start(f32[784,128]{1,0:T(8,128)} %get-tuple-element.24.zdn) | copy-start | bytes 1204228
  8.4 1.3 %collective-permute-start.8 = (f32[11,8,128]{2,1,0:T(8,128)S(1)}, f32[11,8,128]{2,1,0:T(8,128)S(1)}, u32[]{:S(2)}, u32[]{:S(2)}) collective-permute-start(f32[11,8,128]{2,1,0:T(8,128)S(1)} %get-tuple-element.31.mine), channel_id=1, source_target_pairs={{0,1},{1,0},{2,3},{3,2},{4,5},{5,4},{6,7},{7,6},{8,9},{9,8},{10,11... | collective-permute-start | bytes 135176 | tf_op jit(solution)/shard_map/ppermute | solution.py:569
  9.7 5.6 %collective-permute-start.10 = (f32[4,8,128]{2,1,0:T(8,128)S(1)}, f32[4,8,128]{2,1,0:T(8,128)S(1)}, u32[]{:S(2)}, u32[]{:S(2)}) collective-permute-start(f32[4,8,128]{2,1,0:T(8,128)S(1)} %get-tuple-element.33), channel_id=1, source_target_pairs={{0,14},{1,11},{2,8},{3,13},{4,10},{5,15},{6,12},{7,9},{8,22},{9,19... | collective-permute-start | bytes 49160 | tf_op jit(solution)/shard_map/ppermute | solution.py:566
  12.3 9.9 %collective-permute-start.3 = (f32[20,8,128]{2,1,0:T(8,128)S(1)}, f32[20,8,128]{2,1,0:T(8,128)S(1)}, u32[]{:S(2)}, u32[]{:S(2)}) collective-permute-start(f32[20,8,128]{2,1,0:T(8,128)S(1)} %get-tuple-element.25), channel_id=1, source_target_pairs={{0,2},{1,3},{2,4},{3,5},{4,6},{5,7},{6,0},{7,1},{8,10},{9,11},{10,... | collective-permute-start | bytes 245768 | tf_op jit(solution)/shard_map/ppermute | solution.py:566
  15.3 6.1 %collective-permute-start.9 = (f32[10,8,128]{2,1,0:T(8,128)S(1)}, f32[10,8,128]{2,1,0:T(8,128)S(1)}, u32[]{:S(2)}, u32[]{:S(2)}) collective-permute-start(f32[10,8,128]{2,1,0:T(8,128)S(1)} %get-tuple-element.32), channel_id=1, source_target_pairs={{0,30},{1,27},{2,24},{3,29},{4,26},{5,31},{6,28},{7,25},{8,6},{9,3... | collective-permute-start | bytes 122888 | tf_op jit(solution)/shard_map/ppermute | solution.py:566
  21.5 6.0 %collective-permute-start.11 = (f32[14,8,128]{2,1,0:T(8,128)S(1)}, f32[14,8,128]{2,1,0:T(8,128)S(1)}, u32[]{:S(2)}, u32[]{:S(2)}) collective-permute-start(f32[14,8,128]{2,1,0:T(8,128)S(1)} %shard_map.52.got), channel_id=1, source_target_pairs={{0,1},{1,0},{2,3},{3,2},{4,5},{5,4},{6,7},{7,6},{8,9},{9,8},{10,11... | collective-permute-start | bytes 172040 | tf_op jit(solution)/shard_map/ppermute | solution.py:569
  22.2 9.4 %collective-permute-start.4 = (f32[40,8,128]{2,1,0:T(8,128)S(1)}, f32[40,8,128]{2,1,0:T(8,128)S(1)}, u32[]{:S(2)}, u32[]{:S(2)}) collective-permute-start(f32[40,8,128]{2,1,0:T(8,128)S(1)} %get-tuple-element.26), channel_id=1, source_target_pairs={{0,6},{1,7},{2,0},{3,1},{4,2},{5,3},{6,4},{7,5},{8,14},{9,15},{10,... | collective-permute-start | bytes 491528 | tf_op jit(solution)/shard_map/ppermute | solution.py:566
  27.5 12.2 %collective-permute-start.2 = (f32[16,48,128]{2,1,0:T(8,128)S(1)}, f32[16,48,128]{2,1,0:T(8,128)S(1)}, u32[]{:S(2)}, u32[]{:S(2)}) collective-permute-start(f32[16,48,128]{2,1,0:T(8,128)S(1)} %copy-done.2), channel_id=1, source_target_pairs={{1,0},{0,1},{3,2},{2,3},{5,4},{4,5},{7,6},{6,7},{9,8},{8,9},{11,10... | collective-permute-start | bytes 1179656 | tf_op jit(solution)/shard_map/ppermute | solution.py:574
  31.6 8.2 %collective-permute-start.6 = (f32[464,128]{1,0:T(8,128)S(1)}, f32[464,128]{1,0:T(8,128)S(1)}, u32[]{:S(2)}, u32[]{:S(2)}) collective-permute-start(f32[464,128]{1,0:T(8,128)S(1)} %get-tuple-element.23.zup), channel_id=1, source_target_pairs={{0,8},{1,9},{2,10},{3,11},{4,12},{5,13},{6,14},{7,15},{8,16},{9,17... | collective-permute-start | bytes 712712 | tf_op jit(solution)/shard_map/ppermute | solution.py:566
  31.6 12.8 %collective-permute-start.13 = (f32[784,128]{1,0:T(8,128)S(1)}, f32[784,128]{1,0:T(8,128)S(1)}, u32[]{:S(2)}, u32[]{:S(2)}) collective-permute-start(f32[784,128]{1,0:T(8,128)S(1)} %collective-permute-done.7.refs_5_), channel_id=1, source_target_pairs={{1,0},{0,1},{3,2},{2,3},{5,4},{4,5},{7,6},{6,7},{9,8},{8,9},{11,10... | collective-permute-start | bytes 1204232 | tf_op jit(solution)/shard_map/ppermute | solution.py:574
  39.7 1.8 %collective-permute-start.5 = (f32[60,8,128]{2,1,0:T(8,128)S(1)}, f32[60,8,128]{2,1,0:T(8,128)S(1)}, u32[]{:S(2)}, u32[]{:S(2)}) collective-permute-start(f32[60,8,128]{2,1,0:T(8,128)S(1)} %shard_map.50.refs_3_), channel_id=1, source_target_pairs={{1,0},{0,1},{3,2},{2,3},{5,4},{4,5},{7,6},{6,7},{9,8},{8,9},{11,10... | collective-permute-start | bytes 737288 | tf_op jit(solution)/shard_map/ppermute | solution.py:574
  39.7 4.6 %collective-permute-start.12 = (f32[464,128]{1,0:T(8,128)S(1)}, f32[464,128]{1,0:T(8,128)S(1)}, u32[]{:S(2)}, u32[]{:S(2)}) collective-permute-start(f32[464,128]{1,0:T(8,128)S(1)} %collective-permute-done.6.refs_4_), channel_id=1, source_target_pairs={{1,0},{0,1},{3,2},{2,3},{5,4},{4,5},{7,6},{6,7},{9,8},{8,9},{11,10... | collective-permute-start | bytes 712712 | tf_op jit(solution)/shard_map/ppermute | solution.py:574
